TPU v7x, 32 devices: a whole 2x2x4 slice. The times are simulated.
32 devices in a mesh: fsdp: 8 (over y, x, core), tensor: 4 (over z).
Axes of the slice: x: 2, y: 2, z: 4, core: 2. Of those that a mesh axis runs over, the one named last changes fastest.
Arguments:
- block_input: bfloat16 [8192, 2048], P(('fsdp', 'tensor')), may hold values from -6 to 6
- doc_ids: int32 [8, 1024], P('fsdp'), may hold values from 0 to 5, never falling along the last dimension, each value on 1 to 512 neighbouring positions
- w_query: bfloat16 [1, 2048, 2048], P(None, 'fsdp', 'tensor')
- w_keyval: bfloat16 [1, 2048, 8, 128], P(None, 'fsdp', 'tensor')
- w_attn_out: bfloat16 [1, 2048, 2048], P(None, 'tensor', 'fsdp'), may hold values from -0.5 to 0.5
- w_gate_up: bfloat16 [1, 2048, 2, 8192], P(None, 'fsdp', None, 'tensor'), may hold values from -0.125 to 0.125
- w_down: bfloat16 [1, 8192, 2048], P(None, 'tensor', 'fsdp'), may hold values from -0.0625 to 0.0625
- norm_gains: bfloat16 [1, 2, 2048], P(None, None, 'fsdp'), may hold values from 0.5 to 1.5
- out_cotangent: float32 [8192, 2048], P(('fsdp', 'tensor')), may hold values from -6 to 6
Outputs:
- block_output: float32 [8192, 2048], P(('fsdp', 'tensor'))
- grad_input: float32 [8192, 2048], P(('fsdp', 'tensor'))
- grad_w_query: float32 [1, 2048, 2048], P(None, 'fsdp', 'tensor')
- grad_w_keyval: float32 [1, 2048, 8, 128], P(None, 'fsdp', 'tensor')
- grad_w_attn_out: float32 [1, 2048, 2048], P(None, 'tensor', 'fsdp')
- grad_w_gate_up: float32 [1, 2048, 2, 8192], P(None, 'fsdp', None, 'tensor')
- grad_w_down: float32 [1, 8192, 2048], P(None, 'tensor', 'fsdp')
- grad_norm_gains: float32 [1, 2, 2048], P(None, None, 'fsdp')
Inputs may be any that keep to these rules, and one draw needn't show every extreme that they name: `doc_ids`: in each row document numbers never fall, every number of 0 to 5 appears, each document holds 1 to 512 tokens and one holds exactly 512.
All inputs are finite; a program needn't handle non-finite values.
Results may differ from a plain program's by a relative error of at most 0.014.
Values may be sent and summed in bfloat16 or wider, within the bound.
A program may use at most 320 MiB of HBM per device.

v0:
```python
import jax
import jax.numpy as jnp
from jax import lax
from jax.sharding import PartitionSpec as P

MAXLEN = 512
NORM_EPSILON = 1e-05
ROPE_BASE = 500000.0


def norm_apply(residual, gain):
    inverse = lax.rsqrt(jnp.mean(residual * residual, axis=-1, keepdims=True) + NORM_EPSILON)
    return (inverse, (residual * inverse * gain.astype(jnp.float32)).astype(jnp.bfloat16))


def norm_back(residual, inverse, gain, grad_normed):
    scaled = grad_normed * gain.astype(jnp.float32)
    grad_gain = jnp.sum(grad_normed * residual * inverse, axis=0)
    grad_residual = inverse * scaled - residual * inverse * inverse * inverse * jnp.mean(
        scaled * residual, axis=-1, keepdims=True
    )
    return (grad_residual, grad_gain)


def rope_tables(doc_row, head_size):
    places = jnp.arange(doc_row.shape[0], dtype=jnp.int32)
    doc_start = jnp.concatenate([jnp.array([True]), doc_row[1:] != doc_row[:-1]])
    starts = lax.cummax(jnp.where(doc_start, places, 0), axis=0)
    exponent = jnp.arange(head_size // 2, dtype=jnp.float32) * (-2.0 / head_size)
    angles = (places - starts).astype(jnp.float32)[:, None] * jnp.power(ROPE_BASE, exponent)[
        None, :
    ]
    return (jnp.cos(angles), jnp.sin(angles))


def rotate(vectors, cosine, sine_table, direction_sign):
    half_size = vectors.shape[-1] // 2
    table_shape = (vectors.shape[0],) + (1,) * (vectors.ndim - 2) + (half_size,)
    cos_part = cosine.reshape(table_shape)
    sin_part = direction_sign * sine_table.reshape(table_shape)
    first_half = vectors[..., :half_size]
    second = vectors[..., half_size:]
    return jnp.concatenate(
        [first_half * cos_part - second * sin_part, second * cos_part + first_half * sin_part],
        axis=-1,
    )


def block_mask(doc_row, block_start, block_rows, key_low, key_high):
    places = jnp.arange(doc_row.shape[0], dtype=jnp.int32)
    own_docs = doc_row[block_start : block_start + block_rows]
    own_places = places[block_start : block_start + block_rows]
    return (own_docs[:, None] == doc_row[None, key_low:key_high]) & (
        places[None, key_low:key_high] <= own_places[:, None]
    )


def attend_block(query_rows, key_rows, value_rows, allowed, score_scale):
    scores = (
        jnp.einsum("qkgd,skd->kgqs", query_rows, key_rows, preferred_element_type=jnp.float32)
        * score_scale
    )
    scores = jnp.where(allowed[None, None], scores, -jnp.inf)
    row_max = jnp.max(scores, axis=-1, keepdims=True)
    log_total = row_max + jnp.log(jnp.sum(jnp.exp(scores - row_max), axis=-1, keepdims=True))
    probabilities = jnp.exp(scores - log_total).astype(jnp.bfloat16)
    attn_out = jnp.einsum(
        "kgqs,skd->qkgd", probabilities, value_rows, preferred_element_type=jnp.float32
    )
    return (attn_out.astype(jnp.bfloat16), log_total)


def attend_back(
    query_rows, key_rows, value_rows, allowed, log_total, out_rows, grad_out, score_scale
):
    scores = (
        jnp.einsum("qkgd,skd->kgqs", query_rows, key_rows, preferred_element_type=jnp.float32)
        * score_scale
    )
    scores = jnp.where(allowed[None, None], scores, -jnp.inf)
    probabilities = jnp.exp(scores - log_total)
    row_delta = jnp.einsum("qkgd,qkgd->kgq", grad_out, out_rows, preferred_element_type=jnp.float32)
    grad_probs = jnp.einsum(
        "qkgd,skd->kgqs", grad_out, value_rows, preferred_element_type=jnp.float32
    )
    grad_scores = (probabilities * (grad_probs - row_delta[..., None]) * score_scale).astype(
        jnp.bfloat16
    )
    grad_query = jnp.einsum(
        "kgqs,skd->qkgd", grad_scores, key_rows, preferred_element_type=jnp.float32
    )
    grad_key = jnp.einsum(
        "kgqs,qkgd->skd", grad_scores, query_rows, preferred_element_type=jnp.float32
    )
    grad_value = jnp.einsum(
        "kgqs,qkgd->skd",
        probabilities.astype(jnp.bfloat16),
        grad_out,
        preferred_element_type=jnp.float32,
    )
    return (grad_query, grad_key, grad_value)


def per_device(
    block_input,
    doc_ids,
    w_query,
    w_keyval,
    w_attn_out,
    w_gate_up,
    w_down,
    norm_gains,
    out_cotangent,
):
    layers = w_query.shape[0]
    doc_row = doc_ids[0]
    row_count = doc_row.shape[0]
    local_rows = block_input.shape[0]
    kv_local = w_keyval.shape[2]
    head_size = w_keyval.shape[3] // 2
    group_size = w_query.shape[2] // (kv_local * head_size)
    block_rows = min(512, row_count)
    score_scale = head_size ** (-0.5)
    cosine, sine_table = rope_tables(doc_row, head_size)
    block_starts = list(range(0, row_count, block_rows))
    windows = [
        (max(0, block_start - MAXLEN), block_start + block_rows) for block_start in block_starts
    ]
    mask_list = [
        block_mask(
            doc_row, block_start, block_rows, windows[block_index][0], windows[block_index][1]
        )
        for block_index, block_start in enumerate(block_starts)
    ]

    def spread(rows_local):
        return lax.all_gather(rows_local, "tensor", axis=0, tiled=True)

    def collect(term_fn):
        return lax.psum_scatter(
            term_fn(jnp.int32(0), lax.axis_size("tensor") * local_rows).astype(jnp.bfloat16),
            "tensor",
            scatter_dimension=0,
            tiled=True,
        ).astype(jnp.float32)

    def spread_grad(rows_local):
        return lax.all_gather(rows_local, "tensor", axis=0, tiled=True)

    def collect_grad(term_fn):
        return lax.psum_scatter(
            term_fn(jnp.int32(0), lax.axis_size("tensor") * local_rows).astype(jnp.bfloat16),
            "tensor",
            scatter_dimension=0,
            tiled=True,
        ).astype(jnp.float32)

    residual = block_input.astype(jnp.float32)
    layer_index = 0
    weights = (
        lax.all_gather(w_query[layer_index], "fsdp", axis=0, tiled=True),
        lax.all_gather(w_keyval[layer_index], "fsdp", axis=0, tiled=True),
        lax.all_gather(w_attn_out[layer_index], "fsdp", axis=1, tiled=True),
        lax.all_gather(w_gate_up[layer_index], "fsdp", axis=0, tiled=True),
        lax.all_gather(w_down[layer_index], "fsdp", axis=1, tiled=True),
        lax.all_gather(norm_gains[layer_index], "fsdp", axis=1, tiled=True),
    )
    w_query_all, w_keyval_all, w_out_all, w_gate_all, w_down_all, gains_all = weights
    model_width = w_query_all.shape[0]
    inv_attn, normed = norm_apply(residual, gains_all[0])
    normed_all = spread(normed)
    query_full = jnp.dot(normed_all, w_query_all, preferred_element_type=jnp.float32).reshape(
        row_count, kv_local, group_size, head_size
    )
    keyval = jnp.dot(
        normed_all, w_keyval_all.reshape(model_width, -1), preferred_element_type=jnp.float32
    ).reshape(row_count, kv_local, 2 * head_size)
    query_rows = rotate(query_full, cosine, sine_table, 1.0).astype(jnp.bfloat16)
    key_rows = rotate(keyval[..., :head_size], cosine, sine_table, 1.0).astype(jnp.bfloat16)
    value_rows = keyval[..., head_size:].astype(jnp.bfloat16)
    out_list = []
    total_list = []
    for block_index, block_start in enumerate(block_starts):
        key_low, key_high = windows[block_index]
        out_block, log_total = attend_block(
            query_rows[block_start : block_start + block_rows],
            key_rows[key_low:key_high],
            value_rows[key_low:key_high],
            mask_list[block_index],
            score_scale,
        )
        out_list.append(out_block)
        total_list.append(log_total)
    attended = jnp.concatenate(out_list, axis=0).reshape(row_count, -1)

    def attn_term(row_start, row_size):
        return jnp.dot(attended, w_out_all, preferred_element_type=jnp.float32)

    middle = residual + collect(attn_term)
    inv_mlp, normed_mlp = norm_apply(middle, gains_all[1])
    normed_mlp_all = spread(normed_mlp)
    gate_up = jnp.dot(
        normed_mlp_all, w_gate_all.reshape(model_width, -1), preferred_element_type=jnp.float32
    ).reshape(row_count, 2, -1)
    gate_value = gate_up[:, 0]
    up_value = gate_up[:, 1]
    hidden = (jax.nn.silu(gate_value) * up_value).astype(jnp.bfloat16)

    def mlp_term(row_start, row_size):
        return jnp.dot(hidden, w_down_all, preferred_element_type=jnp.float32)

    new_rows = middle + collect(mlp_term)
    stored = [
        (
            residual,
            inv_attn,
            normed_all,
            query_rows,
            key_rows,
            value_rows,
            attended,
            total_list,
            middle,
            inv_mlp,
            normed_mlp_all,
            gate_value,
            up_value,
            hidden,
        )
    ]
    kept_weights = [weights]
    residual = new_rows
    output_rows = residual
    grad_rows = out_cotangent
    layer_grads = [None] * layers
    for layer_index in reversed(range(layers)):
        weights = kept_weights[layer_index]
        w_query_all, w_keyval_all, w_out_all, w_gate_all, w_down_all, gains_all = weights
        model_width = w_query_all.shape[0]
        (
            residual,
            inv_attn,
            normed_all,
            query_rows,
            key_rows,
            value_rows,
            attended,
            total_list,
            middle,
            inv_mlp,
            normed_mlp_all,
            gate_value,
            up_value,
            hidden,
        ) = stored[layer_index]
        grad_all = spread_grad(grad_rows.astype(jnp.bfloat16))
        grad_down = jnp.dot(hidden.T, grad_all, preferred_element_type=jnp.float32)
        grad_hidden = jnp.dot(grad_all, w_down_all.T, preferred_element_type=jnp.float32)
        sigmoid_gate = jax.nn.sigmoid(gate_value)
        grad_gate = (
            grad_hidden * up_value * sigmoid_gate * (1.0 + gate_value * (1.0 - sigmoid_gate))
        )
        grad_up = grad_hidden * jax.nn.silu(gate_value)
        grad_gate_up = (
            jnp.stack([grad_gate, grad_up], axis=1).astype(jnp.bfloat16).reshape(row_count, -1)
        )
        grad_wgu = jnp.dot(
            normed_mlp_all.T, grad_gate_up, preferred_element_type=jnp.float32
        ).reshape(w_gate_all.shape)

        def mlp_back(row_start, row_size):
            return jnp.dot(
                grad_gate_up,
                w_gate_all.reshape(model_width, -1).T,
                preferred_element_type=jnp.float32,
            )

        norm_part, grad_gain_mlp = norm_back(middle, inv_mlp, gains_all[1], collect_grad(mlp_back))
        grad_middle = grad_rows + norm_part
        middle_all = spread_grad(grad_middle.astype(jnp.bfloat16))
        grad_wo = jnp.dot(attended.T, middle_all, preferred_element_type=jnp.float32)
        grad_attended = (
            jnp.dot(middle_all, w_out_all.T, preferred_element_type=jnp.float32)
            .astype(jnp.bfloat16)
            .reshape(row_count, kv_local, group_size, head_size)
        )
        attended_heads = attended.reshape(row_count, kv_local, group_size, head_size)
        grad_keys = jnp.zeros((row_count, kv_local, head_size), jnp.float32)
        grad_values = jnp.zeros((row_count, kv_local, head_size), jnp.float32)
        query_grads = []
        for block_index, block_start in enumerate(block_starts):
            block_stop = block_start + block_rows
            key_low, key_high = windows[block_index]
            grad_query_block, grad_key_part, grad_value_part = attend_back(
                query_rows[block_start:block_stop],
                key_rows[key_low:key_high],
                value_rows[key_low:key_high],
                mask_list[block_index],
                total_list[block_index],
                attended_heads[block_start:block_stop],
                grad_attended[block_start:block_stop],
                score_scale,
            )
            query_grads.append(grad_query_block)
            pad_width = ((key_low, row_count - key_high), (0, 0), (0, 0))
            grad_keys = grad_keys + jnp.pad(grad_key_part, pad_width)
            grad_values = grad_values + jnp.pad(grad_value_part, pad_width)
        grad_query = (
            rotate(jnp.concatenate(query_grads, axis=0), cosine, sine_table, -1.0)
            .astype(jnp.bfloat16)
            .reshape(row_count, -1)
        )
        grad_keyval = (
            jnp.concatenate([rotate(grad_keys, cosine, sine_table, -1.0), grad_values], axis=-1)
            .astype(jnp.bfloat16)
            .reshape(row_count, -1)
        )
        grad_wq = jnp.dot(normed_all.T, grad_query, preferred_element_type=jnp.float32)
        grad_wkv = jnp.dot(normed_all.T, grad_keyval, preferred_element_type=jnp.float32).reshape(
            w_keyval_all.shape
        )

        def attn_back(row_start, row_size):
            return jnp.dot(grad_query, w_query_all.T, preferred_element_type=jnp.float32) + jnp.dot(
                grad_keyval,
                w_keyval_all.reshape(model_width, -1).T,
                preferred_element_type=jnp.float32,
            )

        norm_part, grad_gain_attn = norm_back(
            residual, inv_attn, gains_all[0], collect_grad(attn_back)
        )
        grad_rows = grad_middle + norm_part
        gain_total = lax.psum(jnp.stack([grad_gain_attn, grad_gain_mlp]), "tensor")
        local_set = (grad_wq, grad_wkv, grad_wo, grad_wgu, grad_down, gain_total)
        layer_grads[layer_index] = (
            lax.psum_scatter(
                local_set[0].astype(jnp.bfloat16), "fsdp", scatter_dimension=0, tiled=True
            ).astype(jnp.float32),
            lax.psum_scatter(
                local_set[1].astype(jnp.bfloat16), "fsdp", scatter_dimension=0, tiled=True
            ).astype(jnp.float32),
            lax.psum_scatter(
                local_set[2].astype(jnp.bfloat16), "fsdp", scatter_dimension=1, tiled=True
            ).astype(jnp.float32),
            lax.psum_scatter(
                local_set[3].astype(jnp.bfloat16), "fsdp", scatter_dimension=0, tiled=True
            ).astype(jnp.float32),
            lax.psum_scatter(
                local_set[4].astype(jnp.bfloat16), "fsdp", scatter_dimension=1, tiled=True
            ).astype(jnp.float32),
            lax.psum_scatter(local_set[5], "fsdp", scatter_dimension=1, tiled=True),
        )
    stacked = tuple((jnp.stack([layer_grads[0][member]]) for member in range(6)))
    return (
        output_rows,
        grad_rows,
        stacked[0],
        stacked[1],
        stacked[2],
        stacked[3],
        stacked[4],
        stacked[5],
    )


def solution(mesh):
    return jax.shard_map(
        per_device,
        mesh=mesh,
        in_specs=(
            P(("fsdp", "tensor"), None),
            P("fsdp", None),
            P(None, "fsdp", "tensor"),
            P(None, "fsdp", "tensor", None),
            P(None, "tensor", "fsdp"),
            P(None, "fsdp", None, "tensor"),
            P(None, "tensor", "fsdp"),
            P(None, None, "fsdp"),
            P(("fsdp", "tensor"), None),
        ),
        out_specs=(
            P(("fsdp", "tensor"), None),
            P(("fsdp", "tensor"), None),
            P(None, "fsdp", "tensor"),
            P(None, "fsdp", "tensor", None),
            P(None, "tensor", "fsdp"),
            P(None, "fsdp", None, "tensor"),
            P(None, "tensor", "fsdp"),
            P(None, None, "fsdp"),
        ),
        check_vma=False,
    )
```

profile of v0, /device:TPU:0, one launch (start us, length us, event | category | flops | bytes accessed | tf_op | source)
XLA Modules:
  0.0 1383.0 jit_solution(8392175093084249237)
XLA Ops:
  8.9 10.6 all-gather
  21.0 2.5 fusion.40
  27.7 8.9 all-gather.24.cloned.1.call-done
  38.1 81.4 %all-gather.16.cloned.1.call-done = bf16[1024,2048]{1,0:T(8,128)(2,1)} async-done(((bf16[256,2048]{1,0:T(8,128)(2,1)}), bf16[1024,2048]{1,0:T(8,128)(2,1)}) %all-gather.16.cloned.1.call-update) | async-done | bytes 4194320 | tf_op jit(solution)/shard_map/all_gather | solution.py:137
  119.5 3.5 fusion.97
  123.1 24.6 %all-gather.26.cloned.1.call-done = bf16[1,2048,512]{2,1,0:T(8,128)(2,1)} async-done(((bf16[1,256,512]{2,1,0:T(8,128)(2,1)}), bf16[1,2048,512]{2,1,0:T(8,128)(2,1)}) %all-gather.26.cloned.1.call-update) | async-done | bytes 2097168 | tf_op jit(solution)/shard_map/all_gather | solution.py:161
  147.7 5.2 fusion.59
  153.3 7.6 fusion.8
  160.9 9.2 exponential_reduce_fusion
  173.4 2.5 copy-done.7
  175.9 6.5 convolution_convert_fusion.6
  182.5 4.3 convolution_convert_fusion.5
  187.9 6.0 convolution_convert_fusion.2
  195.5 2.2 copy.55
  197.8 73.2 %reduce-scatter.13.cloned.1.call-done = bf16[256,2048]{1,0:T(8,128)(2,1)} async-done(((bf16[1024,2048]{1,0:T(8,128)(2,1)}), bf16[256,2048]{1,0:T(8,128)(2,1)}) %reduce-scatter.13.cloned.1.call-update) | async-done | bytes 1048592 | tf_op jit(solution)/shard_map/reduce_scatter | solution.py:140
  272.6 2.6 multiply_convert_fusion.1
  277.2 86.4 %all-gather.30.cloned.1.call-done = bf16[1,2048,2,2048]{3,1,2,0:T(8,128)(2,1)} async-done(((bf16[1,256,2,2048]{3,1,2,0:T(8,128)(2,1)}), bf16[1,2048,2,2048]{3,1,2,0:T(8,128)(2,1)}) %all-gather.30.cloned.1.call-update) | async-done | bytes 16777232 | tf_op jit(solution)/shard_map/all_gather | solution.py:164
  363.6 22.6 %copy.56 = bf16[1,2048,2,2048]{1,3,2,0:T(8,128)(2,1)} copy(bf16[1,2048,2,2048]{3,1,2,0:T(8,128)(2,1)} %all-gather.30.cloned.1.call-done) | data formatting | bytes 33554432 | tf_op jit(solution)/shard_map/all_gather | solution.py:164
  386.2 60.3 %all-gather.18.cloned.1.call-done = bf16[1024,2048]{1,0:T(8,128)(2,1)} async-done(((bf16[256,2048]{1,0:T(8,128)(2,1)}), bf16[1024,2048]{1,0:T(8,128)(2,1)}) %all-gather.18.cloned.1.call-update) | async-done | bytes 4194320 | tf_op jit(solution)/shard_map/all_gather | solution.py:137
  446.5 23.7 %fusion = f32[1024,2,2048]{2,0,1:T(8,128)} fusion(bf16[1,2048,2,2048]{1,3,2,0:T(8,128)(2,1)} %copy.56, bf16[1024,2048]{1,0:T(8,128)(2,1)} %all-gather.18.cloned.1.call-done), kind=kOutput, calls=%fused_computation.1 | convolution fusion | flops 17179869184 | bytes 37748736 | tf_op jit(solution)/shard_map/dot_general | solution.py:202
  470.2 57.7 %all-gather.20.cloned.1.call-done = bf16[1024,2048]{1,0:T(8,128)(2,1)} async-done(((bf16[256,2048]{1,0:T(8,128)(2,1)}), bf16[1024,2048]{1,0:T(8,128)(2,1)}) %all-gather.20.cloned.1.call-update) | async-done | bytes 4194320 | tf_op jit(solution)/shard_map/all_gather | solution.py:148
  527.9 56.3 %all-gather.32.cloned.1.call-done = bf16[1,2048,2048]{2,1,0:T(8,128)(2,1)} async-done(((bf16[1,2048,256]{2,1,0:T(8,128)(2,1)}), bf16[1,2048,2048]{2,1,0:T(8,128)(2,1)}) %all-gather.32.cloned.1.call-update) | async-done | bytes 8388624 | tf_op jit(solution)/shard_map/all_gather | solution.py:165
  584.1 20.5 %multiply_bitcast_fusion.1 = (bf16[1024,1,2048]{2,0,1:T(8,128)(2,1)}, bf16[1024,1,2048]{2,0,1:T(8,128)(2,1)}) fusion(f32[1024,2,2048]{2,0,1:T(8,128)} %fusion, bf16[1024,2048]{1,0:T(8,128)(2,1)} %all-gather.20.cloned.1.call-done, bf16[1,2048,2048]{2,1,0:T(8,128)(2,1)} %all-gather.32.cloned.1.call-done), kind=kOutput, calls=%fused_computation.31 | convolution fusion | flops 8617197568 | bytes 37748736 | tf_op jit(solution)/shard_map/dot_general | solution.py:258
  604.6 24.2 %bitcast_convert_fusion = bf16[1024,2048]{1,0:T(8,128)(2,1)} fusion(bf16[1,2048,2,2048]{3,1,2,0:T(8,128)(2,1)} %all-gather.30.cloned.1.call-done, bf16[1024,1,2048]{2,0,1:T(8,128)(2,1)} %get-tuple-element.41, bf16[1024,1,2048]{2,0,1:T(8,128)(2,1)} %get-tuple-element.40), kind=kOutput, calls=%fused_computation.24 | convolution fusion | flops 17186160640 | bytes 29360128 | tf_op jit(solution)/shard_map/dot_general | solution.py:272
  628.9 76.9 %reduce-scatter.17.cloned.1.call-done = bf16[256,2048]{1,0:T(8,128)(2,1)} async-done(((bf16[1024,2048]{1,0:T(8,128)(2,1)}), bf16[256,2048]{1,0:T(8,128)(2,1)}) %reduce-scatter.17.cloned.1.call-update) | async-done | bytes 1048592 | tf_op jit(solution)/shard_map/reduce_scatter | solution.py:151
  705.8 2.1 fusion.49
  708.0 3.2 fusion.95
  711.3 81.3 %all-gather.22.cloned.1.call-done = bf16[1024,2048]{1,0:T(8,128)(2,1)} async-done(((bf16[256,2048]{1,0:T(8,128)(2,1)}), bf16[1024,2048]{1,0:T(8,128)(2,1)}) %all-gather.22.cloned.1.call-update) | async-done | bytes 4194320 | tf_op jit(solution)/shard_map/all_gather | solution.py:148
  792.6 5.2 fusion.62
  799.6 6.3 convolution_bitcast_fusion.4
  806.0 5.5 fusion.13
  811.5 2.1 convolution_bitcast_fusion.5
  813.6 1.8 convolution_bitcast_fusion
  815.4 9.3 fusion.4
  824.7 6.2 convolution_bitcast_fusion.1
  830.9 3.4 fusion.65
  834.4 6.5 fusion.66
  842.2 2.4 subtract_convert_fusion
  844.7 2.4 fusion.57
  847.1 3.4 fusion.10
  850.6 8.0 multiply_convert_fusion
  858.6 2.0 copy-done.14
  860.6 11.5 convolution_convert_fusion.1
  872.2 4.6 fusion.32
  877.3 5.8 convolution_convert_fusion.3
  883.2 6.0 convolution_convert_fusion.4
  889.3 13.9 %fusion.29 = bf16[1024,2048]{1,0:T(8,128)(2,1)} fusion(bf16[1024,2048]{1,0:T(8,128)(2,1)} %copy-done.14, bf16[1,2048,2048]{2,1,0:T(8,128)(2,1)} %all-gather.32.cloned.1.call-done), kind=kOutput, calls=%fused_computation.51 | convolution fusion | flops 8592031744 | bytes 16777216 | tf_op jit(solution)/shard_map/dot_general | solution.py:210
  903.2 7.5 maximum_convert_fusion
  910.8 11.9 copy.65
  922.7 3.3 reduce-scatter.19.cloned.1.call-done
  926.0 1.9 fusion.53
  929.5 24.7 %convolution_convert_fusion = bf16[2048,2,2048]{2,0,1:T(8,128)(2,1)} fusion(bf16[1024,2,2048]{0,2,1:T(8,128)(2,1)} %copy.65, bf16[1024,2048]{1,0:T(8,128)(2,1)} %all-gather.18.cloned.1.call-done), kind=kOutput, calls=%fused_computation.14 | convolution fusion | flops 17188257792 | bytes 29360128 | tf_op jit(solution)/shard_map/dot_general | solution.py:267
  954.3 47.0 %reduce-scatter.29.cloned.1.call-done = bf16[2048,256]{1,0:T(8,128)(2,1)} async-done(((bf16[2048,2048]{1,0:T(8,128)(2,1)}), bf16[2048,256]{1,0:T(8,128)(2,1)}) %reduce-scatter.29.cloned.1.call-update) | async-done | bytes 1048592 | tf_op jit(solution)/shard_map/reduce_scatter | solution.py:349
  1001.3 2.7 bitcast_convert_fusion.2
  1004.0 36.3 %reduce-scatter.23.cloned.1.call-done = bf16[256,2,128]{2,0,1:T(8,128)(2,1)} async-done(((bf16[2048,2,128]{2,0,1:T(8,128)(2,1)}), bf16[256,2,128]{2,0,1:T(8,128)(2,1)}) %reduce-scatter.23.cloned.1.call-update) | async-done | bytes 131088 | tf_op jit(solution)/shard_map/reduce_scatter | solution.py:340
  1042.1 43.0 %reduce-scatter.25.cloned.1.call-done = bf16[512,256]{1,0:T(8,128)(2,1)} async-done(((bf16[512,2048]{1,0:T(8,128)(2,1)}), bf16[512,256]{1,0:T(8,128)(2,1)}) %reduce-scatter.25.cloned.1.call-update) | async-done | bytes 262160 | tf_op jit(solution)/shard_map/reduce_scatter | solution.py:343
  1086.9 43.1 %reduce-scatter.21.cloned.1.call-done = bf16[256,512]{1,0:T(8,128)(2,1)} async-done(((bf16[2048,512]{1,0:T(8,128)(2,1)}), bf16[256,512]{1,0:T(8,128)(2,1)}) %reduce-scatter.21.cloned.1.call-update) | async-done | bytes 262160 | tf_op jit(solution)/shard_map/reduce_scatter | solution.py:337
  1131.8 77.1 %reduce-scatter.15.cloned.1.call-done = bf16[256,2048]{1,0:T(8,128)(2,1)} async-done(((bf16[1024,2048]{1,0:T(8,128)(2,1)}), bf16[256,2048]{1,0:T(8,128)(2,1)}) %reduce-scatter.15.cloned.1.call-update) | async-done | bytes 1048592 | tf_op jit(solution)/shard_map/reduce_scatter | solution.py:140
  1209.0 6.0 fusion.44
  1215.0 34.1 %reduce-scatter.31.cloned.1.call-done = f32[256,2]{1,0:T(8,128)} async-done(((f32[2048,2]{1,0:T(8,128)}), f32[256,2]{1,0:T(8,128)}) %reduce-scatter.31.cloned.1.call-update) | async-done | bytes 2064
  1250.0 12.5 psum.8
  1262.5 106.4 %reduce-scatter.27.cloned.1.call-done = bf16[256,2,2048]{2,0,1:T(8,128)(2,1)} async-done(((bf16[2048,2,2048]{2,0,1:T(8,128)(2,1)}), bf16[256,2,2048]{2,0,1:T(8,128)(2,1)}) %reduce-scatter.27.cloned.1.call-update) | async-done | bytes 2097168 | tf_op jit(solution)/shard_map/reduce_scatter | solution.py:346
  1368.9 2.1 bitcast_convert_fusion.1
  1371.0 5.3 copy.68
  (196 shorter events, 30.9 us)
Async XLA Ops:
  7.2 17.8 %copy-start.36 = (s32[1,1024]{1,0:T(1,128)S(1)}, s32[1,1024]{1,0:T(1,128)}, u32[]{:S(2)}) copy-start(s32[1,1024]{1,0:T(1,128)} %param.11) | copy-start | bytes 12292
  7.2 29.4 %all-gather.24.cloned.1.call-start = ((), (), s32[]{:S(2)}) async-start(), calls=%async_computation.23 | async-start | bytes 1179648 | tf_op jit(solution)/shard_map/all_gather | solution.py:162
  8.8 110.7 %all-gather.16.cloned.1.call-start = ((), (), s32[]{:S(2)}) async-start(), calls=%async_computation.10 | async-start | bytes 5242880 | tf_op jit(solution)/shard_map/all_gather | solution.py:137
  21.0 6.7 copy-start.42
  21.0 6.7 copy-start.34
  21.0 686.9 %copy-start.32 = (f32[1,1,2048]{2,1,0:T(1,128)}, f32[1,1,2048]{2,1,0:T(1,128)S(1)}, u32[]{:S(2)}) copy-start(f32[1,1,2048]{2,1,0:T(1,128)S(1)} %get-tuple-element.54) | copy-start | bytes 24580
  23.6 124.1 %all-gather.26.cloned.1.call-start = ((), (), s32[]{:S(2)}) async-start(), calls=%async_computation.24 | async-start | bytes 2359296 | tf_op jit(solution)/shard_map/all_gather | solution.py:161
  24.3 162.7 %all-gather.28.cloned.1.call-start = ((), (), s32[]{:S(2)}) async-start(), calls=%async_computation.25 | async-start | bytes 2359296 | tf_op jit(solution)/shard_map/all_gather | solution.py:163
  24.9 246.1 %reduce-scatter.13.cloned.1.call-start = ((), (), s32[]{:S(2)}) async-start(), calls=%async_computation.11 | async-start | bytes 5242880 | tf_op jit(solution)/shard_map/reduce_scatter | solution.py:140
  26.9 126.0 %copy-start.16 = (f32[1024,32]{0,1:T(8,128)}, f32[1024,32]{0,1:T(8,128)S(1)}, u32[]{:S(2)}) copy-start(f32[1024,32]{0,1:T(8,128)S(1)} %get-tuple-element.58) | copy-start | bytes 393220
  27.2 148.7 %copy-start.26 = (pred[512,512]{0,1:T(8,128)(4,1)}, pred[512,512]{0,1:T(8,128)(4,1)S(1)}, u32[]{:S(2)}) copy-start(pred[512,512]{0,1:T(8,128)(4,1)S(1)} %compare_and_fusion) | copy-start | bytes 786436
  27.7 154.7 %copy-start.12 = (pred[512,1024]{0,1:T(8,128)(4,1)}, pred[512,1024]{0,1:T(8,128)(4,1)S(1)}, u32[]{:S(2)}) copy-start(pred[512,1024]{0,1:T(8,128)(4,1)S(1)} %fusion.61) | copy-start | bytes 1572868
  123.0 59.5 %copy-start.48 = (bf16[1024,2,128]{0,2,1:T(8,128)(2,1)}, bf16[1024,2,128]{0,2,1:T(8,128)(2,1)S(1)}, u32[]{:S(2)}) copy-start(bf16[1024,2,128]{0,2,1:T(8,128)(2,1)S(1)} %get-tuple-element.61) | copy-start | bytes 1572868
  123.1 47.0 %copy-start.17 = (bf16[1024,2,32]{0,2,1:T(8,128)(2,1)}, bf16[1024,2,32]{0,2,1:T(8,128)(2,1)S(1)}, u32[]{:S(2)}) copy-start(bf16[1024,2,32]{0,2,1:T(8,128)(2,1)S(1)} %get-tuple-element.48) | copy-start | bytes 393220
  123.1 47.0 %copy-start.19 = (bf16[1024,2,32]{0,2,1:T(8,128)(2,1)}, bf16[1024,2,32]{0,2,1:T(8,128)(2,1)S(1)}, u32[]{:S(2)}) copy-start(bf16[1024,2,32]{0,2,1:T(8,128)(2,1)S(1)} %get-tuple-element.49) | copy-start | bytes 393220
  153.3 16.8 %copy-start.8 = (bf16[1024,2,4,32]{0,3,2,1:T(8,128)(2,1)}, bf16[1024,2,4,32]{0,3,2,1:T(8,128)(2,1)S(1)}, u32[]{:S(2)}) copy-start(bf16[1024,2,4,32]{0,3,2,1:T(8,128)(2,1)S(1)} %get-tuple-element.44) | copy-start | bytes 1572868
  153.3 16.8 %copy-start.10 = (bf16[1024,2,4,32]{0,3,2,1:T(8,128)(2,1)}, bf16[1024,2,4,32]{0,3,2,1:T(8,128)(2,1)S(1)}, u32[]{:S(2)}) copy-start(bf16[1024,2,4,32]{0,3,2,1:T(8,128)(2,1)S(1)} %get-tuple-element.45) | copy-start | bytes 1572868
  170.1 12.3 copy-start.39
  170.2 12.3 slice-start
  170.2 12.3 slice-start.1
  171.6 10.8 slice-start.2
  175.9 6.5 copy-start.40
  175.9 6.6 slice-start.3
  182.4 4.4 copy-start.22
  186.8 7.1 copy-start.24
  193.9 77.0 %copy-start = (bf16[256,2048]{1,0:T(8,128)(2,1)S(1)}, bf16[256,2048]{1,0:T(8,128)(2,1)}, u32[]{:S(2)}) copy-start(bf16[256,2048]{1,0:T(8,128)(2,1)} %param.10) | copy-start | bytes 3145732
  194.0 169.6 %all-gather.30.cloned.1.call-start = ((), (), s32[]{:S(2)}) async-start(), calls=%async_computation.26 | async-start | bytes 18874368 | tf_op jit(solution)/shard_map/all_gather | solution.py:164
  197.7 77.6 %copy-start.4 = (f32[256,2048]{1,0:T(8,128)S(1)}, f32[256,2048]{1,0:T(8,128)}, u32[]{:S(2)}) copy-start(f32[256,2048]{1,0:T(8,128)} %param.18) | copy-start | bytes 6291460
  197.7 248.7 %all-gather.18.cloned.1.call-start = ((), (), s32[]{:S(2)}) async-start(), calls=%async_computation.12 | async-start | bytes 5242880 | tf_op jit(solution)/shard_map/all_gather | solution.py:137
  272.6 435.3 %copy-start.37 = (f32[256]{0:T(256)}, f32[256]{0:T(256)S(1)}, u32[]{:S(2)}) copy-start(f32[256]{0:T(256)S(1)} %add_rsqrt_fusion) | copy-start | bytes 3076
  275.2 252.7 %all-gather.20.cloned.1.call-start = ((), (), s32[]{:S(2)}) async-start(), calls=%async_computation.14 | async-start | bytes 5242880 | tf_op jit(solution)/shard_map/all_gather | solution.py:148
  276.4 307.7 %all-gather.32.cloned.1.call-start = ((), (), s32[]{:S(2)}) async-start(), calls=%async_computation.27 | async-start | bytes 9437184 | tf_op jit(solution)/shard_map/all_gather | solution.py:165
  277.2 428.6 %reduce-scatter.17.cloned.1.call-start = ((), (), s32[]{:S(2)}) async-start(), calls=%async_computation.15 | async-start | bytes 5242880 | tf_op jit(solution)/shard_map/reduce_scatter | solution.py:151
  628.9 77.0 %copy-start.2 = (bf16[256,2048]{1,0:T(8,128)(2,1)S(1)}, bf16[256,2048]{1,0:T(8,128)(2,1)}, u32[]{:S(2)}) copy-start(bf16[256,2048]{1,0:T(8,128)(2,1)} %reduce-scatter.13.cloned.1.call-done) | copy-start | bytes 3145732
  628.9 163.7 %all-gather.22.cloned.1.call-start = ((), (), s32[]{:S(2)}) async-start(), calls=%async_computation.16 | async-start | bytes 5242880 | tf_op jit(solution)/shard_map/all_gather | solution.py:148
  707.9 89.9 %copy-start.44 = (f32[256]{0:T(256)}, f32[256]{0:T(256)S(1)}, u32[]{:S(2)}) copy-start(f32[256]{0:T(256)S(1)} %broadcast_multiply_fusion.2) | copy-start | bytes 3076
  711.2 86.7 %copy-start.23 = (bf16[2,64,4,512]{3,1,2,0:T(8,128)(2,1)S(1)}, bf16[2,64,4,512]{3,1,2,0:T(8,128)(2,1)}, u32[]{:S(2)}) copy-start(bf16[2,64,4,512]{3,1,2,0:T(8,128)(2,1)} %copy-done.22) | copy-start | bytes 1572868
  711.2 86.7 %copy-start.25 = (bf16[2,64,4,512]{3,1,2,0:T(8,128)(2,1)S(1)}, bf16[2,64,4,512]{3,1,2,0:T(8,128)(2,1)}, u32[]{:S(2)}) copy-start(bf16[2,64,4,512]{3,1,2,0:T(8,128)(2,1)} %copy-done.24) | copy-start | bytes 1572868
  711.2 88.4 %copy-start.27 = (pred[512,512]{0,1:T(8,128)(4,1)S(1)}, pred[512,512]{0,1:T(8,128)(4,1)}, u32[]{:S(2)}) copy-start(pred[512,512]{0,1:T(8,128)(4,1)} %copy-done.26) | copy-start | bytes 786436
  711.2 88.4 %copy-start.41 = (f32[1,8,512]{2,1,0:T(8,128)S(1)}, f32[1,8,512]{2,1,0:T(8,128)}, u32[]{:S(2)}) copy-start(f32[1,8,512]{2,1,0:T(8,128)} %copy-done.40) | copy-start | bytes 49156
  711.2 214.7 %reduce-scatter.19.cloned.1.call-start = ((), (), s32[]{:S(2)}) async-start(), calls=%async_computation.17 | async-start | bytes 5242880 | tf_op jit(solution)/shard_map/reduce_scatter | solution.py:151
  799.6 15.8 %slice-start.4 = ((s8[16777216]{0:T(1024)(128)(4,1)}), s8[4194304]{0:T(1024)(128)(4,1)S(1)}, s32[]{:S(2)}) async-start(s8[16777216]{0:T(1024)(128)(4,1)} %bitcast.277), calls=%async_computation.33 | async-start | bytes 8388608
  799.6 15.8 %slice-start.5 = ((s8[16777216]{0:T(1024)(128)(4,1)}), s8[4194304]{0:T(1024)(128)(4,1)S(1)}, s32[]{:S(2)}) async-start(s8[16777216]{0:T(1024)(128)(4,1)} %bitcast.277), calls=%async_computation.34 | async-start | bytes 8388608
  805.9 5.5 copy-start.9
  806.0 5.5 copy-start.11
  806.0 9.5 slice-start.6
  824.7 6.2 copy-start.1
  824.7 6.2 copy-start.30
  850.6 150.7 %reduce-scatter.29.cloned.1.call-start = ((), (), s32[]{:S(2)}) async-start(), calls=%async_computation.22 | async-start | bytes 9437184 | tf_op jit(solution)/shard_map/reduce_scatter | solution.py:349
  850.6 10.0 copy-start.46
  872.1 5.2 copy-start.29
  872.1 168.2 %reduce-scatter.23.cloned.1.call-start = ((), (), s32[]{:S(2)}) async-start(), calls=%async_computation.19 | async-start | bytes 1179648 | tf_op jit(solution)/shard_map/reduce_scatter | solution.py:340
  876.8 208.3 %reduce-scatter.25.cloned.1.call-start = ((), (), s32[]{:S(2)}) async-start(), calls=%async_computation.20 | async-start | bytes 2359296 | tf_op jit(solution)/shard_map/reduce_scatter | solution.py:343
  883.2 246.9 %reduce-scatter.21.cloned.1.call-start = ((), (), s32[]{:S(2)}) async-start(), calls=%async_computation.18 | async-start | bytes 2359296 | tf_op jit(solution)/shard_map/reduce_scatter | solution.py:337
  889.2 319.7 %reduce-scatter.15.cloned.1.call-start = ((), (), s32[]{:S(2)}) async-start(), calls=%async_computation.13 | async-start | bytes 5242880 | tf_op jit(solution)/shard_map/reduce_scatter | solution.py:140
  903.2 345.9 %reduce-scatter.31.cloned.1.call-start = ((), (), s32[]{:S(2)}) async-start(), calls=%async_computation.28 | async-start | bytes 1179648
  910.8 15.2 %copy-start.35 = (f32[1,1,2048]{2,1,0:T(1,128)S(1)}, f32[1,1,2048]{2,1,0:T(1,128)}, u32[]{:S(2)}) copy-start(f32[1,1,2048]{2,1,0:T(1,128)} %copy-done.34) | copy-start | bytes 24580
  910.8 15.2 %copy-start.43 = (f32[256]{0:T(256)S(1)}, f32[256]{0:T(256)}, u32[]{:S(2)}) copy-start(f32[256]{0:T(256)} %copy-done.42) | copy-start | bytes 3076
  929.3 439.6 %reduce-scatter.27.cloned.1.call-start = ((), (), s32[]{:S(2)}) async-start(), calls=%async_computation.21 | async-start | bytes 18874368 | tf_op jit(solution)/shard_map/reduce_scatter | solution.py:346
  954.2 254.7 %copy-start.3 = (bf16[256,2048]{1,0:T(8,128)(2,1)S(1)}, bf16[256,2048]{1,0:T(8,128)(2,1)}, u32[]{:S(2)}) copy-start(bf16[256,2048]{1,0:T(8,128)(2,1)} %reduce-scatter.13.cloned.1.call-done) | copy-start | bytes 3145732
  954.2 254.7 %copy-start.6 = (bf16[256,2048]{1,0:T(8,128)(2,1)S(1)}, bf16[256,2048]{1,0:T(8,128)(2,1)}, u32[]{:S(2)}) copy-start(bf16[256,2048]{1,0:T(8,128)(2,1)} %reduce-scatter.17.cloned.1.call-done) | copy-start | bytes 3145732
  954.2 254.7 %copy-start.33 = (f32[1,1,2048]{2,1,0:T(1,128)S(1)}, f32[1,1,2048]{2,1,0:T(1,128)}, u32[]{:S(2)}) copy-start(f32[1,1,2048]{2,1,0:T(1,128)} %copy-done.32) | copy-start | bytes 24580
  954.2 254.7 %copy-start.38 = (f32[256]{0:T(256)S(1)}, f32[256]{0:T(256)}, u32[]{:S(2)}) copy-start(f32[256]{0:T(256)} %copy-done.37) | copy-start | bytes 3076
  954.3 254.7 %copy-start.45 = (f32[256]{0:T(256)S(1)}, f32[256]{0:T(256)}, u32[]{:S(2)}) copy-start(f32[256]{0:T(256)} %copy-done.44) | copy-start | bytes 3076
  (12 other events, 31.8 us)
Sparse Core Ops, SparseCore 0:
  10.5 26.0 all-gather.23
  38.7 80.7 all-gather.15
  121.4 26.2 all-gather.25
  149.4 28.0 all-gather.27
  194.1 76.8 reduce-scatter.12
  273.3 90.2 all-gather.29
  365.7 80.7 all-gather.17
  448.6 79.2 all-gather.19
  529.8 54.3 all-gather.31
  629.0 76.7 reduce-scatter.16
  711.3 81.2 all-gather.21
  850.7 75.2 reduce-scatter.18
  929.4 71.7 reduce-scatter.28
  1004.3 35.9 reduce-scatter.22
  1044.0 41.1 reduce-scatter.24
  1088.9 41.1 reduce-scatter.20
  1132.2 76.7 reduce-scatter.14
  1212.6 36.4 reduce-scatter.30
  1252.6 116.1 reduce-scatter.26
where the time goes:
time: 1390 us; the launch traced here: 1380 us
  waiting for transfers between devices  999 us (72%)
  matrix products  221 us (16%)
  other arithmetic  67 us (5%)
  local copies, waits for them, and re-layouts  55.7 us (4%)
  blocking collectives  23 us (2%)
  between operations  15.1 us (1%)
    reduce_scatter x2, waiting for transfers between devices, collect(): lax.psum_scatter(term_fn(jnp.int32(0), lax.axis_size('tensor') * local_ro...  150 us
    all_gather x2, waiting for transfers between devices, spread(): return lax.all_gather(rows_local, 'tensor', axis=0, tiled=True)  142 us
    all_gather x2, waiting for transfers between devices, spread_grad(): return lax.all_gather(rows_local, 'tensor', axis=0, tiled=True)  139 us
    reduce_scatter x1, waiting for transfers between devices, per_device(): lax.psum_scatter(local_set[3].astype(jnp.bfloat16), 'fsdp', scatter_dimen...  106 us
    all_gather x1, waiting for transfers between devices, per_device(): lax.all_gather(w_gate_up[layer_index], 'fsdp', axis=0, tiled=True)  86.4 us
    reduce_scatter x2, waiting for transfers between devices, collect_grad(): lax.psum_scatter(term_fn(jnp.int32(0), lax.axis_size('tensor') * local_ro...  80.2 us
    all_gather x1, waiting for transfers between devices, per_device(): lax.all_gather(w_down[layer_index], 'fsdp', axis=1, tiled=True)  56.3 us
    reduce_scatter x1, waiting for transfers between devices, per_device(): lax.psum_scatter(local_set[4].astype(jnp.bfloat16), 'fsdp', scatter_dimen...  47 us
  transfers between devices with their start and end apart: 19, of which 18 were waited for; matrix products, arithmetic and copies ran while one was open for 15% of the time, Pallas kernels for 0%

commit v1 on v0

--- a/solution.py
+++ b/solution.py
@@ -6,6 +6,18 @@
 MAXLEN = 512
 NORM_EPSILON = 1e-05
 ROPE_BASE = 500000.0
+
+
+def gather_by_bits(value, axis, dim):
+    ways, here = (lax.axis_size(axis), lax.axis_index(axis))
+    grown, reach = (value, 1)
+    while reach < ways:
+        theirs = lax.ppermute(grown, axis, [(d, d ^ reach) for d in range(ways)])
+        mine_first = jnp.concatenate([grown, theirs], axis=dim)
+        theirs_first = jnp.concatenate([theirs, grown], axis=dim)
+        grown = jnp.where(here & reach == 0, mine_first, theirs_first)
+        reach = 2 * reach
+    return grown
 
 
 def norm_apply(residual, gain):
@@ -134,7 +146,7 @@
     ]
 
     def spread(rows_local):
-        return lax.all_gather(rows_local, "tensor", axis=0, tiled=True)
+        return gather_by_bits(rows_local, "tensor", 0)
 
     def collect(term_fn):
         return lax.psum_scatter(

time: 1390 us -> 1330 us (0.957)
  waiting for transfers between devices: 999 us -> 920 us
    ppermute x0 -> x4, waiting for transfers between devices: none -> 184 us  [gather_by_bits(): theirs = lax.ppermute(grown, axis, [(d, d ^ reach) for d in range(ways)])]
    all_gather x2 -> x0, waiting for transfers between devices: 142 us -> none  [spread(): return lax.all_gather(rows_local, 'tensor', axis=0, tiled=True)]
    all_gather x2, waiting for transfers between devices: 139 us -> 81.3 us  [spread_grad(): return lax.all_gather(rows_local, 'tensor', axis=0, tiled=True)]
    all_gather x1, waiting for transfers between devices: 86.4 us -> 60.3 us  [per_device(): lax.all_gather(w_gate_up[layer_index], 'fsdp', axis=0, tiled=True)]
    all_gather x1, waiting for transfers between devices: 24.6 us -> 0.02 us  [per_device(): lax.all_gather(w_query[layer_index], 'fsdp', axis=0, tiled=True)]
    unnamed x20 -> x18, waiting for transfers between devices: 36.3 us -> 35.7 us
  transfers between devices with their start and end apart: 19 -> 21, of which waited for: 18 -> 16; matrix products, arithmetic and copies ran while one was open for 15% -> 17% of each run, Pallas kernels for 0% -> 0%
where the time goes in v1:
time: 1330 us; the launch traced here: 1320 us
  waiting for transfers between devices  920 us (69%)
  matrix products  228 us (17%)
  other arithmetic  68.6 us (5%)
  local copies, waits for them, and re-layouts  55.6 us (4%)
  blocking collectives  22.8 us (2%)
  between operations  15 us (1%)
    ppermute x4, waiting for transfers between devices, gather_by_bits(): theirs = lax.ppermute(grown, axis, [(d, d ^ reach) for d in range(ways)])  184 us
    reduce_scatter x2, waiting for transfers between devices, collect(): lax.psum_scatter(term_fn(jnp.int32(0), lax.axis_size('tensor') * local_ro...  148 us
    reduce_scatter x1, waiting for transfers between devices, per_device(): lax.psum_scatter(local_set[3].astype(jnp.bfloat16), 'fsdp', scatter_dimen...  106 us
    all_gather x2, waiting for transfers between devices, spread_grad(): return lax.all_gather(rows_local, 'tensor', axis=0, tiled=True)  81.3 us
    reduce_scatter x2, waiting for transfers between devices, collect_grad(): lax.psum_scatter(term_fn(jnp.int32(0), lax.axis_size('tensor') * local_ro...  76.9 us
    all_gather x1, waiting for transfers between devices, per_device(): lax.all_gather(w_gate_up[layer_index], 'fsdp', axis=0, tiled=True)  60.3 us
    all_gather x1, waiting for transfers between devices, per_device(): lax.all_gather(w_down[layer_index], 'fsdp', axis=1, tiled=True)  57.1 us
    reduce_scatter x1, waiting for transfers between devices, per_device(): lax.psum_scatter(local_set[4].astype(jnp.bfloat16), 'fsdp', scatter_dimen...  47.3 us
  transfers between devices with their start and end apart: 21, of which 16 were waited for; matrix products, arithmetic and copies ran while one was open for 17% of the time, Pallas kernels for 0%

profile of v1, /device:TPU:0, one launch (start us, length us, event | category | flops | bytes accessed | tf_op | source)
XLA Modules:
  0.0 1320.9 jit_solution(15715131205385203739)
XLA Ops:
  9.6 10.6 all-gather
  25.5 23.8 %collective-permute-done = bf16[256,2048]{1,0:T(8,128)(2,1)S(1)} collective-permute-done((bf16[256,2048]{1,0:T(8,128)(2,1)S(1)}, bf16[256,2048]{1,0:T(8,128)(2,1)S(1)}, u32[]{:S(2)}, u32[]{:S(2)}) %collective-permute-start) | collective-permute-done | bytes 1048608 | tf_op jit(solution)/shard_map/ppermute | solution.py:15
  49.4 2.3 maximum_select_fusion.2
  51.7 2.6 collective-permute-start.1
  58.8 86.1 %collective-permute-done.1 = bf16[512,2048]{1,0:T(8,128)(2,1)} collective-permute-done((bf16[512,2048]{1,0:T(8,128)(2,1)}, bf16[512,2048]{1,0:T(8,128)(2,1)}, u32[]{:S(2)}, u32[]{:S(2)}) %collective-permute-start.1) | collective-permute-done | bytes 2097184 | tf_op jit(solution)/shard_map/ppermute | solution.py:15
  144.8 5.2 fusion.100
  150.2 6.5 fusion.60
  157.1 7.5 fusion.8
  164.6 9.2 exponential_reduce_fusion
  177.0 2.5 copy-done.7
  179.6 6.3 convolution_convert_fusion.6
  186.0 4.3 convolution_convert_fusion.5
  190.5 6.4 convolution_convert_fusion.2
  196.9 3.9 copy.55
  202.9 71.1 %reduce-scatter.13.cloned.1.call-done = bf16[256,2048]{1,0:T(8,128)(2,1)} async-done(((bf16[1024,2048]{1,0:T(8,128)(2,1)}), bf16[256,2048]{1,0:T(8,128)(2,1)}) %reduce-scatter.13.cloned.1.call-update) | async-done | bytes 1048592 | tf_op jit(solution)/shard_map/reduce_scatter | solution.py:152
  278.9 23.1 %collective-permute-done.2 = bf16[256,2048]{1,0:T(8,128)(2,1)S(1)} collective-permute-done((bf16[256,2048]{1,0:T(8,128)(2,1)S(1)}, bf16[256,2048]{1,0:T(8,128)(2,1)S(1)}, u32[]{:S(2)}, u32[]{:S(2)}) %collective-permute-start.2) | collective-permute-done | bytes 1048608 | tf_op jit(solution)/shard_map/ppermute | solution.py:15
  303.0 3.2 collective-permute-start.3
  306.2 60.3 %all-gather.24.cloned.1.call-done = bf16[1,2048,2,2048]{3,1,2,0:T(8,128)(2,1)} async-done(((bf16[1,256,2,2048]{3,1,2,0:T(8,128)(2,1)}), bf16[1,2048,2,2048]{3,1,2,0:T(8,128)(2,1)}) %all-gather.24.cloned.1.call-update) | async-done | bytes 16777232 | tf_op jit(solution)/shard_map/all_gather | solution.py:176
  366.6 22.6 %copy.56 = bf16[1,2048,2,2048]{1,3,2,0:T(8,128)(2,1)} copy(bf16[1,2048,2,2048]{3,1,2,0:T(8,128)(2,1)} %all-gather.24.cloned.1.call-done) | data formatting | bytes 33554432 | tf_op jit(solution)/shard_map/all_gather | solution.py:176
  389.1 51.2 %collective-permute-done.3 = bf16[512,2048]{1,0:T(8,128)(2,1)} collective-permute-done((bf16[512,2048]{1,0:T(8,128)(2,1)S(1)}, bf16[512,2048]{1,0:T(8,128)(2,1)}, u32[]{:S(2)}, u32[]{:S(2)}) %collective-permute-start.3) | collective-permute-done | bytes 2097184 | tf_op jit(solution)/shard_map/ppermute | solution.py:15
  440.3 24.6 %fusion = f32[1024,2,2048]{2,0,1:T(8,128)} fusion(bf16[1,2048,2,2048]{1,3,2,0:T(8,128)(2,1)} %copy.56, bf16[512,2048]{1,0:T(8,128)(2,1)} %collective-permute-done.3, bf16[512,2048]{1,0:T(8,128)(2,1)S(1)} %maximum_select_fusion.3, pred[]{:T(512)S(6)} %eq.46), kind=kOutput, calls=%fused_computation.1 | convolution fusion | flops 17198743552 | bytes 37748736 | tf_op jit(solution)/shard_map/dot_general | solution.py:214
  464.9 57.1 %all-gather.26.cloned.1.call-done = bf16[1,2048,2048]{2,1,0:T(8,128)(2,1)} async-done(((bf16[1,2048,256]{2,1,0:T(8,128)(2,1)}), bf16[1,2048,2048]{2,1,0:T(8,128)(2,1)}) %all-gather.26.cloned.1.call-update) | async-done | bytes 8388624 | tf_op jit(solution)/shard_map/all_gather | solution.py:177
  522.1 20.5 %multiply_bitcast_fusion.1 = (bf16[1024,1,2048]{2,0,1:T(8,128)(2,1)}, bf16[1024,1,2048]{2,0,1:T(8,128)(2,1)}) fusion(f32[1024,2,2048]{2,0,1:T(8,128)} %fusion, bf16[1024,2048]{1,0:T(8,128)(2,1)} %all-gather.14.cloned.1.call-done, bf16[1,2048,2048]{2,1,0:T(8,128)(2,1)} %all-gather.26.cloned.1.call-done), kind=kOutput, calls=%fused_computation.31 | convolution fusion | flops 8617197568 | bytes 37748736 | tf_op jit(solution)/shard_map/dot_general | solution.py:270
  542.5 24.2 %bitcast_convert_fusion = bf16[1024,2048]{1,0:T(8,128)(2,1)} fusion(bf16[1,2048,2,2048]{3,1,2,0:T(8,128)(2,1)} %all-gather.24.cloned.1.call-done, bf16[1024,1,2048]{2,0,1:T(8,128)(2,1)} %get-tuple-element.41, bf16[1024,1,2048]{2,0,1:T(8,128)(2,1)} %get-tuple-element.40), kind=kOutput, calls=%fused_computation.24 | convolution fusion | flops 17186160640 | bytes 29360128 | tf_op jit(solution)/shard_map/dot_general | solution.py:284
  566.9 76.9 %reduce-scatter.17.cloned.1.call-done = bf16[256,2048]{1,0:T(8,128)(2,1)} async-done(((bf16[1024,2048]{1,0:T(8,128)(2,1)}), bf16[256,2048]{1,0:T(8,128)(2,1)}) %reduce-scatter.17.cloned.1.call-update) | async-done | bytes 1048592 | tf_op jit(solution)/shard_map/reduce_scatter | solution.py:163
  643.8 2.1 fusion.50
  645.9 3.2 fusion.98
  649.2 81.3 %all-gather.16.cloned.1.call-done = bf16[1024,2048]{1,0:T(8,128)(2,1)} async-done(((bf16[256,2048]{1,0:T(8,128)(2,1)}), bf16[1024,2048]{1,0:T(8,128)(2,1)}) %all-gather.16.cloned.1.call-update) | async-done | bytes 4194320 | tf_op jit(solution)/shard_map/all_gather | solution.py:160
  730.6 5.2 fusion.63
  737.6 6.3 convolution_bitcast_fusion.4
  743.9 5.5 fusion.13
  749.4 2.1 convolution_bitcast_fusion.5
  751.5 1.8 convolution_bitcast_fusion
  753.4 9.3 fusion.4
  762.7 6.2 convolution_bitcast_fusion.1
  768.9 3.4 fusion.66
  772.3 6.5 fusion.67
  780.2 2.4 subtract_convert_fusion
  782.7 2.4 fusion.58
  785.1 3.4 fusion.10
  788.6 8.0 multiply_convert_fusion
  796.6 2.0 copy-done.14
  798.6 11.5 convolution_convert_fusion.1
  810.6 6.7 fusion.33
  817.4 5.8 convolution_convert_fusion.3
  823.3 7.2 convolution_convert_fusion.4
  830.6 13.9 %fusion.28 = bf16[1024,2048]{1,0:T(8,128)(2,1)} fusion(bf16[1024,2048]{1,0:T(8,128)(2,1)} %copy-done.14, bf16[1,2048,2048]{2,1,0:T(8,128)(2,1)} %all-gather.26.cloned.1.call-done), kind=kOutput, calls=%fused_computation.52 | convolution fusion | flops 8592031744 | bytes 16777216 | tf_op jit(solution)/shard_map/dot_general | solution.py:222
  844.6 7.6 maximum_convert_fusion
  852.2 11.9 copy.65
  864.1 2.0 fusion.54
  867.8 24.1 %convolution_convert_fusion = bf16[2048,2,2048]{2,0,1:T(8,128)(2,1)} fusion(bf16[1024,2,2048]{0,2,1:T(8,128)(2,1)} %copy.65, bf16[512,2048]{1,0:T(8,128)(2,1)} %collective-permute-done.3, bf16[512,2048]{1,0:T(8,128)(2,1)S(1)} %copy-done.22, pred[]{:T(512)S(6)} %eq.46), kind=kOutput, calls=%fused_computation.14 | convolution fusion | flops 17207132160 | bytes 29360128 | tf_op jit(solution)/shard_map/dot_general | solution.py:279
  892.0 47.3 %reduce-scatter.29.cloned.1.call-done = bf16[2048,256]{1,0:T(8,128)(2,1)} async-done(((bf16[2048,2048]{1,0:T(8,128)(2,1)}), bf16[2048,256]{1,0:T(8,128)(2,1)}) %reduce-scatter.29.cloned.1.call-update) | async-done | bytes 1048592 | tf_op jit(solution)/shard_map/reduce_scatter | solution.py:361
  939.3 2.7 bitcast_convert_fusion.2
  942.0 36.3 %reduce-scatter.23.cloned.1.call-done = bf16[256,2,128]{2,0,1:T(8,128)(2,1)} async-done(((bf16[2048,2,128]{2,0,1:T(8,128)(2,1)}), bf16[256,2,128]{2,0,1:T(8,128)(2,1)}) %reduce-scatter.23.cloned.1.call-update) | async-done | bytes 131088 | tf_op jit(solution)/shard_map/reduce_scatter | solution.py:352
  980.1 43.2 %reduce-scatter.25.cloned.1.call-done = bf16[512,256]{1,0:T(8,128)(2,1)} async-done(((bf16[512,2048]{1,0:T(8,128)(2,1)}), bf16[512,256]{1,0:T(8,128)(2,1)}) %reduce-scatter.25.cloned.1.call-update) | async-done | bytes 262160 | tf_op jit(solution)/shard_map/reduce_scatter | solution.py:355
  1025.0 43.1 %reduce-scatter.21.cloned.1.call-done = bf16[256,512]{1,0:T(8,128)(2,1)} async-done(((bf16[2048,512]{1,0:T(8,128)(2,1)}), bf16[256,512]{1,0:T(8,128)(2,1)}) %reduce-scatter.21.cloned.1.call-update) | async-done | bytes 262160 | tf_op jit(solution)/shard_map/reduce_scatter | solution.py:349
  1068.1 1.8 bitcast_convert_fusion.4
  1069.9 77.1 %reduce-scatter.15.cloned.1.call-done = bf16[256,2048]{1,0:T(8,128)(2,1)} async-done(((bf16[1024,2048]{1,0:T(8,128)(2,1)}), bf16[256,2048]{1,0:T(8,128)(2,1)}) %reduce-scatter.15.cloned.1.call-update) | async-done | bytes 1048592 | tf_op jit(solution)/shard_map/reduce_scatter | solution.py:152
  1147.1 6.0 fusion.45
  1153.1 34.1 %reduce-scatter.31.cloned.1.call-done = f32[256,2]{1,0:T(8,128)} async-done(((f32[2048,2]{1,0:T(8,128)}), f32[256,2]{1,0:T(8,128)}) %reduce-scatter.31.cloned.1.call-update) | async-done | bytes 2064
  1188.1 12.2 psum.8
  1200.4 106.4 %reduce-scatter.27.cloned.1.call-done = bf16[256,2,2048]{2,0,1:T(8,128)(2,1)} async-done(((bf16[2048,2,2048]{2,0,1:T(8,128)(2,1)}), bf16[256,2,2048]{2,0,1:T(8,128)(2,1)}) %reduce-scatter.27.cloned.1.call-update) | async-done | bytes 2097168 | tf_op jit(solution)/shard_map/reduce_scatter | solution.py:358
  1306.8 2.1 bitcast_convert_fusion.1
  1308.9 5.3 copy.68
  (194 shorter events, 34.2 us)
Async XLA Ops:
  7.2 47.2 %copy-start.35 = (s32[1,1024]{1,0:T(1,128)S(1)}, s32[1,1024]{1,0:T(1,128)}, u32[]{:S(2)}) copy-start(s32[1,1024]{1,0:T(1,128)} %param.11) | copy-start | bytes 12292
  7.2 49.9 %all-gather.18.cloned.1.call-start = ((), (), s32[]{:S(2)}) async-start(), calls=%async_computation.21 | async-start | bytes 1179648 | tf_op jit(solution)/shard_map/all_gather | solution.py:174
  8.8 141.4 %all-gather.20.cloned.1.call-start = ((), (), s32[]{:S(2)}) async-start(), calls=%async_computation.22 | async-start | bytes 2359296 | tf_op jit(solution)/shard_map/all_gather | solution.py:173
  9.6 180.9 %all-gather.22.cloned.1.call-start = ((), (), s32[]{:S(2)}) async-start(), calls=%async_computation.23 | async-start | bytes 2359296 | tf_op jit(solution)/shard_map/all_gather | solution.py:175
  21.7 37.1 %copy-start.39 = (f32[256]{0:T(256)}, f32[256]{0:T(256)S(1)}, u32[]{:S(2)}) copy-start(f32[256]{0:T(256)S(1)} %add_rsqrt_fusion.1) | copy-start | bytes 3076
  21.8 624.1 %copy-start.31 = (f32[1,1,2048]{2,1,0:T(1,128)}, f32[1,1,2048]{2,1,0:T(1,128)S(1)}, u32[]{:S(2)}) copy-start(f32[1,1,2048]{2,1,0:T(1,128)S(1)} %get-tuple-element.54) | copy-start | bytes 24580
  23.9 25.5 %collective-permute-start = (bf16[256,2048]{1,0:T(8,128)(2,1)S(1)}, bf16[256,2048]{1,0:T(8,128)(2,1)S(1)}, u32[]{:S(2)}, u32[]{:S(2)}) collective-permute-start(bf16[256,2048]{1,0:T(8,128)(2,1)S(1)} %fusion.41), channel_id=1, source_target_pairs={{0,1},{1,0},{2,3},{3,2},{4,5},{5,4},{6,7},{7,6},{8,9},{9,8},{10,11... | collective-permute-start | bytes 3145736 | tf_op jit(solution)/shard_map/ppermute | solution.py:15
  51.7 93.2 %collective-permute-start.1 = (bf16[512,2048]{1,0:T(8,128)(2,1)}, bf16[512,2048]{1,0:T(8,128)(2,1)}, u32[]{:S(2)}, u32[]{:S(2)}) collective-permute-start(bf16[512,2048]{1,0:T(8,128)(2,1)} %maximum_select_fusion.2), channel_id=1, source_target_pairs={{0,2},{1,3},{2,0},{3,1},{4,6},{5,7},{6,4},{7,5},{8,10},{9,11},{10,... | collective-permute-start | bytes 6291464 | tf_op jit(solution)/shard_map/ppermute | solution.py:15
  54.3 219.7 %reduce-scatter.13.cloned.1.call-start = ((), (), s32[]{:S(2)}) async-start(), calls=%async_computation.10 | async-start | bytes 5242880 | tf_op jit(solution)/shard_map/reduce_scatter | solution.py:152
  56.6 100.1 %copy-start.16 = (f32[1024,32]{0,1:T(8,128)}, f32[1024,32]{0,1:T(8,128)S(1)}, u32[]{:S(2)}) copy-start(f32[1024,32]{0,1:T(8,128)S(1)} %get-tuple-element.58) | copy-start | bytes 393220
  57.1 128.8 %copy-start.12 = (pred[512,1024]{0,1:T(8,128)(4,1)}, pred[512,1024]{0,1:T(8,128)(4,1)S(1)}, u32[]{:S(2)}) copy-start(pred[512,1024]{0,1:T(8,128)(4,1)S(1)} %fusion.62) | copy-start | bytes 1572868
  150.2 23.6 %copy-start.17 = (bf16[1024,2,32]{0,2,1:T(8,128)(2,1)}, bf16[1024,2,32]{0,2,1:T(8,128)(2,1)S(1)}, u32[]{:S(2)}) copy-start(bf16[1024,2,32]{0,2,1:T(8,128)(2,1)S(1)} %get-tuple-element.48) | copy-start | bytes 393220
  150.2 23.6 %copy-start.19 = (bf16[1024,2,32]{0,2,1:T(8,128)(2,1)}, bf16[1024,2,32]{0,2,1:T(8,128)(2,1)S(1)}, u32[]{:S(2)}) copy-start(bf16[1024,2,32]{0,2,1:T(8,128)(2,1)S(1)} %get-tuple-element.49) | copy-start | bytes 393220
  157.1 16.7 %copy-start.8 = (bf16[1024,2,4,32]{0,3,2,1:T(8,128)(2,1)}, bf16[1024,2,4,32]{0,3,2,1:T(8,128)(2,1)S(1)}, u32[]{:S(2)}) copy-start(bf16[1024,2,4,32]{0,3,2,1:T(8,128)(2,1)S(1)} %get-tuple-element.44) | copy-start | bytes 1572868
  157.1 16.7 %copy-start.10 = (bf16[1024,2,4,32]{0,3,2,1:T(8,128)(2,1)}, bf16[1024,2,4,32]{0,3,2,1:T(8,128)(2,1)S(1)}, u32[]{:S(2)}) copy-start(bf16[1024,2,4,32]{0,3,2,1:T(8,128)(2,1)S(1)} %get-tuple-element.45) | copy-start | bytes 1572868
  173.8 12.1 copy-start.38
  173.8 12.1 slice-start
  173.8 12.1 slice-start.1
  175.3 4.3 copy-start.7
  175.3 4.3 copy-start.45
  175.3 10.7 slice-start.2
  179.6 6.4 slice-start.3
  185.9 4.4 copy-start.23
  190.3 6.6 copy-start.25
  190.4 6.4 copy-start.27
  196.9 4.1 copy-start.4
  196.9 169.7 %all-gather.24.cloned.1.call-start = ((), (), s32[]{:S(2)}) async-start(), calls=%async_computation.24 | async-start | bytes 18874368 | tf_op jit(solution)/shard_map/all_gather | solution.py:176
  200.8 73.1 %copy-start = (bf16[256,2048]{1,0:T(8,128)(2,1)S(1)}, bf16[256,2048]{1,0:T(8,128)(2,1)}, u32[]{:S(2)}) copy-start(bf16[256,2048]{1,0:T(8,128)(2,1)} %param.10) | copy-start | bytes 3145732
  200.9 264.1 %all-gather.14.cloned.1.call-start = ((), (), s32[]{:S(2)}) async-start(), calls=%async_computation.12 | async-start | bytes 5242880 | tf_op jit(solution)/shard_map/all_gather | solution.py:160
  202.1 320.0 %all-gather.26.cloned.1.call-start = ((), (), s32[]{:S(2)}) async-start(), calls=%async_computation.25 | async-start | bytes 9437184 | tf_op jit(solution)/shard_map/all_gather | solution.py:177
  202.8 440.9 %reduce-scatter.17.cloned.1.call-start = ((), (), s32[]{:S(2)}) async-start(), calls=%async_computation.13 | async-start | bytes 5242880 | tf_op jit(solution)/shard_map/reduce_scatter | solution.py:163
  275.6 370.3 %copy-start.36 = (f32[256]{0:T(256)}, f32[256]{0:T(256)S(1)}, u32[]{:S(2)}) copy-start(f32[256]{0:T(256)S(1)} %add_rsqrt_fusion) | copy-start | bytes 3076
  277.3 24.6 %collective-permute-start.2 = (bf16[256,2048]{1,0:T(8,128)(2,1)S(1)}, bf16[256,2048]{1,0:T(8,128)(2,1)S(1)}, u32[]{:S(2)}, u32[]{:S(2)}) collective-permute-start(bf16[256,2048]{1,0:T(8,128)(2,1)S(1)} %multiply_convert_fusion.1), channel_id=1, source_target_pairs={{0,1},{1,0},{2,3},{3,2},{4,5},{5,4},{6,7},{7,6},{8,9},{9,8},{10,11... | collective-permute-start | bytes 3145736 | tf_op jit(solution)/shard_map/ppermute | solution.py:15
  303.0 137.4 %copy-start.21 = (bf16[512,2048]{1,0:T(8,128)(2,1)}, bf16[512,2048]{1,0:T(8,128)(2,1)S(1)}, u32[]{:S(2)}) copy-start(bf16[512,2048]{1,0:T(8,128)(2,1)S(1)} %maximum_select_fusion.3) | copy-start | bytes 6291460
  303.0 137.3 %collective-permute-start.3 = (bf16[512,2048]{1,0:T(8,128)(2,1)S(1)}, bf16[512,2048]{1,0:T(8,128)(2,1)}, u32[]{:S(2)}, u32[]{:S(2)}) collective-permute-start(bf16[512,2048]{1,0:T(8,128)(2,1)S(1)} %maximum_select_fusion.3), channel_id=1, source_target_pairs={{0,2},{1,3},{2,0},{3,1},{4,6},{5,7},{6,4},{7,5},{8,10},{9,11},{10,... | collective-permute-start | bytes 6291464 | tf_op jit(solution)/shard_map/ppermute | solution.py:15
  566.8 77.0 %copy-start.2 = (bf16[256,2048]{1,0:T(8,128)(2,1)S(1)}, bf16[256,2048]{1,0:T(8,128)(2,1)}, u32[]{:S(2)}) copy-start(bf16[256,2048]{1,0:T(8,128)(2,1)} %reduce-scatter.13.cloned.1.call-done) | copy-start | bytes 3145732
  566.8 163.8 %all-gather.16.cloned.1.call-start = ((), (), s32[]{:S(2)}) async-start(), calls=%async_computation.14 | async-start | bytes 5242880 | tf_op jit(solution)/shard_map/all_gather | solution.py:160
  645.9 84.7 %copy-start.41 = (f32[256]{0:T(256)}, f32[256]{0:T(256)S(1)}, u32[]{:S(2)}) copy-start(f32[256]{0:T(256)S(1)} %broadcast_multiply_fusion.2) | copy-start | bytes 3076
  649.2 86.6 %copy-start.24 = (bf16[2,64,4,512]{3,1,2,0:T(8,128)(2,1)S(1)}, bf16[2,64,4,512]{3,1,2,0:T(8,128)(2,1)}, u32[]{:S(2)}) copy-start(bf16[2,64,4,512]{3,1,2,0:T(8,128)(2,1)} %copy-done.23) | copy-start | bytes 1572868
  649.2 86.6 %copy-start.26 = (bf16[2,64,4,512]{3,1,2,0:T(8,128)(2,1)S(1)}, bf16[2,64,4,512]{3,1,2,0:T(8,128)(2,1)}, u32[]{:S(2)}) copy-start(bf16[2,64,4,512]{3,1,2,0:T(8,128)(2,1)} %copy-done.25) | copy-start | bytes 1572868
  649.2 214.9 %reduce-scatter.19.cloned.1.call-start = ((), (), s32[]{:S(2)}) async-start(), calls=%async_computation.15 | async-start | bytes 5242880 | tf_op jit(solution)/shard_map/reduce_scatter | solution.py:163
  737.5 15.8 %slice-start.4 = ((s8[16777216]{0:T(1024)(128)(4,1)}), s8[4194304]{0:T(1024)(128)(4,1)S(1)}, s32[]{:S(2)}) async-start(s8[16777216]{0:T(1024)(128)(4,1)} %bitcast.274), calls=%async_computation.31 | async-start | bytes 8388608
  737.6 15.8 %slice-start.5 = ((s8[16777216]{0:T(1024)(128)(4,1)}), s8[4194304]{0:T(1024)(128)(4,1)S(1)}, s32[]{:S(2)}) async-start(s8[16777216]{0:T(1024)(128)(4,1)} %bitcast.274), calls=%async_computation.32 | async-start | bytes 8388608
  743.9 5.5 copy-start.9
  743.9 5.5 copy-start.11
  743.9 9.5 slice-start.6
  762.7 6.2 copy-start.1
  762.7 6.2 copy-start.29
  788.5 150.7 %reduce-scatter.29.cloned.1.call-start = ((), (), s32[]{:S(2)}) async-start(), calls=%async_computation.20 | async-start | bytes 9437184 | tf_op jit(solution)/shard_map/reduce_scatter | solution.py:361
  788.6 10.0 copy-start.43
  810.1 7.3 copy-start.28
  810.1 168.2 %reduce-scatter.23.cloned.1.call-start = ((), (), s32[]{:S(2)}) async-start(), calls=%async_computation.17 | async-start | bytes 1179648 | tf_op jit(solution)/shard_map/reduce_scatter | solution.py:352
  817.3 206.0 %reduce-scatter.25.cloned.1.call-start = ((), (), s32[]{:S(2)}) async-start(), calls=%async_computation.18 | async-start | bytes 2359296 | tf_op jit(solution)/shard_map/reduce_scatter | solution.py:355
  823.2 244.9 %reduce-scatter.21.cloned.1.call-start = ((), (), s32[]{:S(2)}) async-start(), calls=%async_computation.16 | async-start | bytes 2359296 | tf_op jit(solution)/shard_map/reduce_scatter | solution.py:349
  830.5 316.5 %reduce-scatter.15.cloned.1.call-start = ((), (), s32[]{:S(2)}) async-start(), calls=%async_computation.11 | async-start | bytes 5242880 | tf_op jit(solution)/shard_map/reduce_scatter | solution.py:152
  844.5 342.7 %reduce-scatter.31.cloned.1.call-start = ((), (), s32[]{:S(2)}) async-start(), calls=%async_computation.26 | async-start | bytes 1179648
  852.2 11.9 copy-start.34
  852.2 11.9 copy-start.40
  867.5 439.3 %reduce-scatter.27.cloned.1.call-start = ((), (), s32[]{:S(2)}) async-start(), calls=%async_computation.19 | async-start | bytes 18874368 | tf_op jit(solution)/shard_map/reduce_scatter | solution.py:358
  891.9 255.1 %copy-start.3 = (bf16[256,2048]{1,0:T(8,128)(2,1)S(1)}, bf16[256,2048]{1,0:T(8,128)(2,1)}, u32[]{:S(2)}) copy-start(bf16[256,2048]{1,0:T(8,128)(2,1)} %reduce-scatter.13.cloned.1.call-done) | copy-start | bytes 3145732
  891.9 255.1 %copy-start.6 = (bf16[256,2048]{1,0:T(8,128)(2,1)S(1)}, bf16[256,2048]{1,0:T(8,128)(2,1)}, u32[]{:S(2)}) copy-start(bf16[256,2048]{1,0:T(8,128)(2,1)} %reduce-scatter.17.cloned.1.call-done) | copy-start | bytes 3145732
  892.0 255.1 %copy-start.32 = (f32[1,1,2048]{2,1,0:T(1,128)S(1)}, f32[1,1,2048]{2,1,0:T(1,128)}, u32[]{:S(2)}) copy-start(f32[1,1,2048]{2,1,0:T(1,128)} %copy-done.31) | copy-start | bytes 24580
  892.0 255.1 %copy-start.37 = (f32[256]{0:T(256)S(1)}, f32[256]{0:T(256)}, u32[]{:S(2)}) copy-start(f32[256]{0:T(256)} %copy-done.36) | copy-start | bytes 3076
  892.0 255.1 %copy-start.42 = (f32[256]{0:T(256)S(1)}, f32[256]{0:T(256)}, u32[]{:S(2)}) copy-start(f32[256]{0:T(256)} %copy-done.41) | copy-start | bytes 3076
  (11 other events, 29.2 us)
Sparse Core Ops, SparseCore 0:
  10.5 26.0 all-gather.17
  38.5 27.7 all-gather.19
  68.2 28.0 all-gather.21
  197.0 76.9 reduce-scatter.12
  276.3 90.2 all-gather.23
  368.5 95.6 all-gather.13
  466.1 55.8 all-gather.25
  566.9 76.7 reduce-scatter.16
  649.3 81.2 all-gather.15
  788.6 75.2 reduce-scatter.18
  867.4 71.7 reduce-scatter.28
  942.3 35.9 reduce-scatter.22
  982.1 41.1 reduce-scatter.24
  1027.0 41.0 reduce-scatter.20
  1070.2 76.7 reduce-scatter.14
  1150.7 36.4 reduce-scatter.30
  1190.6 116.1 reduce-scatter.26
